TPU v7x, 32 devices: a whole 2x2x4 slice. The times are simulated.
32 devices in a mesh: dp: 8 (over y, x, core), vocab: 4 (over z).
Axes of the slice: x: 2, y: 2, z: 4, core: 2. Of those that a mesh axis runs over, the one named last changes fastest.
Arguments:
- hidden: float32 [16, 4608], P('dp'), may hold values from -6 to 6
- norm_gain: float32 [4608], replicated, may hold values from 0.5 to 1.5
- embed_table: bfloat16 [12288, 4608], P(('dp', 'vocab')), as said below
- tokens: int32 [16, 3], replicated, may hold values from 0 to 12287, as said below
Outputs:
- log_probs: float32 [16, 3], P('dp')
- final_hidden: float32 [16, 4608], P('dp')
Inputs may be any that keep to these rules, and one draw needn't show every extreme that they name: `tokens`: token ids are vocabulary entries. `embed_table`: entries lie between -21 / sqrt(4608) and 21 / sqrt(4608).
All inputs are finite; a program needn't handle non-finite values.
Results may differ from a plain program's by a relative error of at most 0.0003.
Values may be sent and summed in bfloat16 or wider, within the bound.
A program may use at most 64 MiB of HBM per device.

v0:
```python
import math
import jax
import jax.numpy as jnp
from jax import lax
from jax.sharding import PartitionSpec as P

D = 4608
STEPS = 3
epsilon_value = 1e-06
softcap_value = 30.0


def project_rows(normed, embed_table):
    return lax.dot_general(
        normed, embed_table, (((1,), (1,)), ((), ())), preferred_element_type=jnp.float32
    )


def on_device(hidden, norm_gain, embed_table, tokens):
    own_rows = hidden.shape[0]
    shard_rows = embed_table.shape[0]
    own_start = lax.axis_index("dp") * own_rows
    shard_start = (
        lax.axis_index("dp") * lax.axis_size("vocab") + lax.axis_index("vocab")
    ) * shard_rows
    scale_factor = math.sqrt(D)
    local_ids = jnp.transpose(tokens) - shard_start
    columns = lax.broadcasted_iota(jnp.int32, (1, 1, shard_rows), 2)
    matches = local_ids[:, :, None] == columns
    onehot = matches.astype(jnp.bfloat16)
    found = jnp.einsum("sbv,vd->sbd", onehot, embed_table, preferred_element_type=jnp.float32)
    current = hidden
    partial_value = lax.psum_scatter(
        found.astype(jnp.bfloat16), "dp", scatter_dimension=1, tiled=True
    )
    summed = lax.psum(partial_value, "vocab").astype(jnp.float32)
    results = []
    for decode_step in range(STEPS):
        square_mean = jnp.mean(current * current, axis=-1, keepdims=True)
        normed = (current * lax.rsqrt(square_mean + epsilon_value) * norm_gain).astype(jnp.bfloat16)
        logits = project_rows(lax.all_gather(normed, "dp", axis=0, tiled=True), embed_table)
        capped = softcap_value * jnp.tanh(logits / softcap_value)
        exp_total = jnp.sum(jnp.exp(capped), axis=-1)
        target = jnp.sum(jnp.where(matches[decode_step], capped, 0.0), axis=-1)
        exp_total, target = lax.psum((exp_total, target), ("dp", "vocab"))
        exp_total = lax.dynamic_slice_in_dim(exp_total, own_start, own_rows, 0)
        target = lax.dynamic_slice_in_dim(target, own_start, own_rows, 0)
        results.append(target - jnp.log(exp_total))
        current = current + scale_factor * summed[decode_step]
    return (jnp.stack(results, axis=1), current)


def solution(mesh):
    return jax.shard_map(
        on_device,
        mesh=mesh,
        in_specs=(P("dp", None), P(), P(("dp", "vocab"), None), P()),
        out_specs=(P("dp", None), P("dp", None)),
        check_vma=False,
    )
```

profile of v0, /device:TPU:12, one launch (start us, length us, event | category | flops | bytes accessed | tf_op | source)
XLA Modules:
  0.0 184.4 jit_solution(427541426465696467)
XLA Ops:
  7.2 0.0 copy-start
  7.2 0.0 copy-start.3
  7.2 0.0 all-reduce.4.cloned.1.call-start
  7.2 0.8 subtract_bitcast_fusion
  8.1 1.1 copy-done
  9.2 1.5 convolution_convert_fusion
  10.7 0.0 all-reduce.4.cloned.1.call-update
  10.8 0.0 copy-done.3
  10.8 0.6 dynamic-slice
  12.0 0.7 iota_compare_fusion
  12.7 53.5 %all-reduce.4.cloned.1.call-done = bf16[3,16,4608]{2,1,0:T(8,128)(2,1)} async-done(((bf16[3,16,4608]{2,1,0:T(8,128)(2,1)}), bf16[3,16,4608]{2,1,0:T(8,128)(2,1)}) %all-reduce.4.cloned.1.call-update) | async-done | bytes 442384
  66.2 1.6 constant_dynamic-slice_fusion
  67.8 17.1 %psum.51 = bf16[3,2,4608]{2,1,0:T(2,128)(2,1)} all-reduce(bf16[3,2,4608]{2,1,0:T(2,128)(2,1)} %constant_dynamic-slice_fusion), channel_id=1, replica_groups=mesh['dp'=8,'vocab'=4] {'vocab'}, use_global_device_ids=true, to_apply=%region_6.7 | all-reduce | flops 27648 | bytes 110592 | tf_op jit(solution)/shard_map/psum | solution.py:36
  85.0 0.9 convert_element_type.18
  85.8 1.6 fusion.8
  87.4 0.2 multiply_reduce_fusion
  87.6 1.5 fusion.14
  89.1 9.8 %all-gather.2 = bf16[8,2,4608]{2,1,0:T(2,128)(2,1)} all-gather(bf16[1,2,4608]{2,1,0:T(2,128)(2,1)S(1)} %get-tuple-element.27), channel_id=1, replica_groups=mesh['dp'=8,'vocab'=4] {'dp'}, dimensions={0}, use_global_device_ids=true | all-gather | bytes 165888 | tf_op jit(solution)/shard_map/all_gather | solution.py:41
  99.0 1.6 reshape.41
  100.6 2.6 %fusion.2 = f32[16,384]{1,0:T(8,128)} fusion(bf16[16,4608]{1,0:T(8,128)(2,1)} %reshape.41, bf16[384,4608]{1,0:T(8,128)(2,1)S(1)} %copy-done), kind=kOutput, calls=%fused_computation.4 | convolution fusion | flops 56635392 | bytes 3710976 | tf_op jit(solution)/shard_map/dot_general | solution.py:14
  103.2 0.0 copy-done.2
  103.2 9.6 %all-gather.1 = bf16[8,2,4608]{2,1,0:T(2,128)(2,1)} all-gather(bf16[1,2,4608]{2,1,0:T(2,128)(2,1)S(1)} %copy-done.2), channel_id=1, replica_groups=mesh['dp'=8,'vocab'=4] {'dp'}, dimensions={0}, use_global_device_ids=true | all-gather | bytes 165888 | tf_op jit(solution)/shard_map/all_gather | solution.py:41
  112.8 1.6 reshape.39
  114.4 2.6 %fusion.4 = f32[16,384]{1,0:T(8,128)} fusion(bf16[16,4608]{1,0:T(8,128)(2,1)} %reshape.39, bf16[384,4608]{1,0:T(8,128)(2,1)S(1)} %copy-done), kind=kOutput, calls=%fused_computation.7 | convolution fusion | flops 56635392 | bytes 3710976 | tf_op jit(solution)/shard_map/dot_general | solution.py:14
  117.0 9.8 %all-gather = bf16[8,2,4608]{2,1,0:T(2,128)(2,1)} all-gather(bf16[1,2,4608]{2,1,0:T(2,128)(2,1)S(1)} %copy-done.1), channel_id=1, replica_groups=mesh['dp'=8,'vocab'=4] {'dp'}, dimensions={0}, use_global_device_ids=true | all-gather | bytes 165888 | tf_op jit(solution)/shard_map/all_gather | solution.py:41
  126.8 1.6 reshape.37
  128.4 2.8 %select_reduce_fusion.2 = (f32[16]{0:T(128)S(1)}, f32[16]{0:T(128)S(1)}, f32[16]{0:T(128)S(1)}, f32[16]{0:T(128)S(1)}, f32[16]{0:T(128)}, /*index=5*/f32[16]{0:T(128)}) fusion(pred[3,16,384]{2,1,0:T(8,128)(4,1)} %iota_compare_fusion, f32[16,384]{1,0:T(8,128)} %fusion.2, f32[16,384]{1,0:T(8,128)} %fusion.4, bf16[16,4608]{1,0:T(8,128)(2,1)} %reshape.37, ...), kind=kOutput, calls=%fused_computation.32 | convolution fusion | flops 56690592 | bytes 3754368 | tf_op jit(solution)/shard_map/dot_general | solution.py:14
  131.2 43.4 %all-reduce.1 = (f32[16]{0:T(128)}, f32[16]{0:T(128)}, f32[16]{0:T(128)}, f32[16]{0:T(128)}, f32[16]{0:T(128)}, /*index=5*/f32[16]{0:T(128)}) all-reduce(f32[16]{0:T(128)S(1)} %get-tuple-element.12, f32[16]{0:T(128)S(1)} %get-tuple-element.13, f32[16]{0:T(128)} %get-tuple-element.14, ...), channel_id=1, replica_groups=mesh['dp'=8,'vocab'=4] {'dp','vocab'}, use_global_device_ids=true, to_apply=%region_16.17 | all-reduce | flops 96 | bytes 768 | tf_op jit(solution)/shard_map/psum | solution.py:45
  174.7 0.7 subtract_bitcast_fusion.3
  175.4 0.7 subtract_bitcast_fusion.2
  176.1 0.8 subtract_bitcast_fusion.1
  176.9 0.7 copy.7
  (7 shorter events, 0.0 us)
Async XLA Ops:
  7.2 2.0 %copy-start = (bf16[384,4608]{1,0:T(8,128)(2,1)S(1)}, bf16[384,4608]{1,0:T(8,128)(2,1)}, u32[]{:S(2)}) copy-start(bf16[384,4608]{1,0:T(8,128)(2,1)} %param.6) | copy-start | bytes 10616836
  7.2 3.6 %copy-start.3 = (u32[32]{0:T(128)S(1)}, u32[32]{0:T(128)}, u32[]{:S(2)}) copy-start(u32[32]{0:T(128)} %constant.39) | copy-start | bytes 388
  7.2 59.0 %all-reduce.4.cloned.1.call-start = ((), (), s32[]{:S(2)}) async-start(), calls=%async_computation | async-start | bytes 884736
  100.6 2.6 %copy-start.2 = (bf16[1,2,4608]{2,1,0:T(2,128)(2,1)S(1)}, bf16[1,2,4608]{2,1,0:T(2,128)(2,1)}, u32[]{:S(2)}) copy-start(bf16[1,2,4608]{2,1,0:T(2,128)(2,1)} %get-tuple-element.26) | copy-start | bytes 55300
  114.4 2.6 %copy-start.1 = (bf16[1,2,4608]{2,1,0:T(2,128)(2,1)S(1)}, bf16[1,2,4608]{2,1,0:T(2,128)(2,1)}, u32[]{:S(2)}) copy-start(bf16[1,2,4608]{2,1,0:T(2,128)(2,1)} %get-tuple-element.28) | copy-start | bytes 55300
Sparse Core Ops, SparseCore 0:
  11.1 55.0 all-reduce.3
where the time goes:
time: 185 us; the launch traced here: 184 us
  blocking collectives  89.8 us (49%)
  waiting for transfers between devices  53.6 us (29%)
  between operations  14.8 us (8%)
  matrix products  9.52 us (5%)
  local copies, waits for them, and re-layouts  8.82 us (5%)
  other arithmetic  7.92 us (4%)
    unnamed x2, waiting for transfers between devices  53.6 us
    psum x1, blocking collectives, on_device(): exp_total, target = lax.psum((exp_total, target), ('dp', 'vocab'))  43.4 us
    all_gather x3, blocking collectives, on_device(): lax.all_gather(normed, 'dp', axis=0, tiled=True)  29.2 us
    psum x1, blocking collectives, on_device(): summed = lax.psum(partial_value, 'vocab').astype(jnp.float32)  17.1 us
    unnamed x14, local copies, waits for them, and re-layouts  8.82 us
    dot_general x3, matrix products, project_rows(): lax.dot_general(normed, embed_table, (((1,), (1,)), ((), ())), preferred_...  7.99 us
  transfers between devices with their start and end apart: 1, of which 1 were waited for; matrix products, arithmetic and copies ran while one was open for 1% of the time, Pallas kernels for 0%

commit v1 on v0

--- a/solution.py
+++ b/solution.py
@@ -8,6 +8,11 @@
 STEPS = 3
 epsilon_value = 1e-06
 softcap_value = 30.0
+
+
+def axis_by_axis(array, inner_axis, outer_axis):
+    half = lax.psum(array, inner_axis)
+    return lax.psum(half, outer_axis)
 
 
 def project_rows(normed, embed_table):
@@ -42,7 +47,7 @@
         capped = softcap_value * jnp.tanh(logits / softcap_value)
         exp_total = jnp.sum(jnp.exp(capped), axis=-1)
         target = jnp.sum(jnp.where(matches[decode_step], capped, 0.0), axis=-1)
-        exp_total, target = lax.psum((exp_total, target), ("dp", "vocab"))
+        exp_total, target = axis_by_axis((exp_total, target), "vocab", "dp")
         exp_total = lax.dynamic_slice_in_dim(exp_total, own_start, own_rows, 0)
         target = lax.dynamic_slice_in_dim(target, own_start, own_rows, 0)
         results.append(target - jnp.log(exp_total))

time: 185 us -> 167 us (0.903)
  blocking collectives: 89.8 us -> 71.9 us
    psum x1 -> x2, blocking collectives: 43.4 us -> 25.5 us  [the longest x1 13.1 us: axis_by_axis(): half = lax.psum(array, inner_axis)]
where the time goes in v1:
time: 167 us; the launch traced here: 165 us
  blocking collectives  71.9 us (43%)
  waiting for transfers between devices  53.6 us (32%)
  between operations  14.8 us (9%)
  matrix products  9.52 us (6%)
  local copies, waits for them, and re-layouts  8.83 us (5%)
  other arithmetic  6.52 us (4%)
    unnamed x2, waiting for transfers between devices  53.6 us
    all_gather x3, blocking collectives, on_device(): lax.all_gather(normed, 'dp', axis=0, tiled=True)  29.2 us
    psum x1, blocking collectives, on_device(): summed = lax.psum(partial_value, 'vocab').astype(jnp.float32)  17.1 us
    psum x1, blocking collectives, axis_by_axis(): half = lax.psum(array, inner_axis)  13.1 us
    psum x1, blocking collectives, axis_by_axis(): return lax.psum(half, outer_axis)  12.4 us
    unnamed x14, local copies, waits for them, and re-layouts  8.83 us
    dot_general x3, matrix products, project_rows(): lax.dot_general(normed, embed_table, (((1,), (1,)), ((), ())), preferred_...  7.99 us
  transfers between devices with their start and end apart: 1, of which 1 were waited for; matrix products, arithmetic and copies ran while one was open for 1% of the time, Pallas kernels for 0%

profile of v1, /device:TPU:12, one launch (start us, length us, event | category | flops | bytes accessed | tf_op | source)
XLA Modules:
  0.0 165.1 jit_solution(7500615834331544840)
XLA Ops:
  7.2 0.0 copy-start
  7.2 0.0 copy-start.3
  7.2 0.0 all-reduce.5.cloned.1.call-start
  7.2 0.8 subtract_bitcast_fusion
  8.1 1.1 copy-done
  9.2 1.5 convolution_convert_fusion
  10.7 0.0 all-reduce.5.cloned.1.call-update
  10.8 0.0 copy-done.3
  10.8 0.6 dynamic-slice
  12.0 0.7 iota_compare_fusion
  12.7 53.5 %all-reduce.5.cloned.1.call-done = bf16[3,16,4608]{2,1,0:T(8,128)(2,1)} async-done(((bf16[3,16,4608]{2,1,0:T(8,128)(2,1)}), bf16[3,16,4608]{2,1,0:T(8,128)(2,1)}) %all-reduce.5.cloned.1.call-update) | async-done | bytes 442384
  66.2 1.6 constant_dynamic-slice_fusion
  67.8 17.1 %psum.95 = bf16[3,2,4608]{2,1,0:T(2,128)(2,1)} all-reduce(bf16[3,2,4608]{2,1,0:T(2,128)(2,1)} %constant_dynamic-slice_fusion), channel_id=1, replica_groups=mesh['dp'=8,'vocab'=4] {'vocab'}, use_global_device_ids=true, to_apply=%region_8.9 | all-reduce | flops 27648 | bytes 110592 | tf_op jit(solution)/shard_map/psum | solution.py:41
  85.0 0.9 convert_element_type.18
  85.8 1.6 fusion.8
  87.4 0.2 multiply_reduce_fusion
  87.6 1.5 fusion.14
  89.1 9.8 %all-gather.2 = bf16[8,2,4608]{2,1,0:T(2,128)(2,1)} all-gather(bf16[1,2,4608]{2,1,0:T(2,128)(2,1)S(1)} %get-tuple-element.33), channel_id=1, replica_groups=mesh['dp'=8,'vocab'=4] {'dp'}, dimensions={0}, use_global_device_ids=true | all-gather | bytes 165888 | tf_op jit(solution)/shard_map/all_gather | solution.py:46
  99.0 1.6 reshape.41
  100.6 2.6 %fusion.2 = f32[16,384]{1,0:T(8,128)} fusion(bf16[16,4608]{1,0:T(8,128)(2,1)} %reshape.41, bf16[384,4608]{1,0:T(8,128)(2,1)S(1)} %copy-done), kind=kOutput, calls=%fused_computation.4 | convolution fusion | flops 56635392 | bytes 3710976 | tf_op jit(solution)/shard_map/dot_general | solution.py:19
  103.2 9.6 %all-gather.1 = bf16[8,2,4608]{2,1,0:T(2,128)(2,1)} all-gather(bf16[1,2,4608]{2,1,0:T(2,128)(2,1)S(1)} %copy-done.2), channel_id=1, replica_groups=mesh['dp'=8,'vocab'=4] {'dp'}, dimensions={0}, use_global_device_ids=true | all-gather | bytes 165888 | tf_op jit(solution)/shard_map/all_gather | solution.py:46
  112.8 1.6 reshape.39
  114.4 2.6 %fusion.4 = f32[16,384]{1,0:T(8,128)} fusion(bf16[16,4608]{1,0:T(8,128)(2,1)} %reshape.39, bf16[384,4608]{1,0:T(8,128)(2,1)S(1)} %copy-done), kind=kOutput, calls=%fused_computation.7 | convolution fusion | flops 56635392 | bytes 3710976 | tf_op jit(solution)/shard_map/dot_general | solution.py:19
  117.0 9.8 %all-gather = bf16[8,2,4608]{2,1,0:T(2,128)(2,1)} all-gather(bf16[1,2,4608]{2,1,0:T(2,128)(2,1)S(1)} %copy-done.1), channel_id=1, replica_groups=mesh['dp'=8,'vocab'=4] {'dp'}, dimensions={0}, use_global_device_ids=true | all-gather | bytes 165888 | tf_op jit(solution)/shard_map/all_gather | solution.py:46
  126.8 1.6 reshape.37
  128.4 2.8 %select_reduce_fusion.2 = (f32[16]{0:T(128)S(1)}, f32[16]{0:T(128)S(1)}, f32[16]{0:T(128)S(1)}, f32[16]{0:T(128)S(1)}, f32[16]{0:T(128)}, /*index=5*/f32[16]{0:T(128)}) fusion(pred[3,16,384]{2,1,0:T(8,128)(4,1)} %iota_compare_fusion, f32[16,384]{1,0:T(8,128)} %fusion.2, f32[16,384]{1,0:T(8,128)} %fusion.4, bf16[16,4608]{1,0:T(8,128)(2,1)} %reshape.37, ...), kind=kOutput, calls=%fused_computation.32 | convolution fusion | flops 56690592 | bytes 3754368 | tf_op jit(solution)/shard_map/dot_general | solution.py:19
  131.2 13.1 %all-reduce.2 = (f32[16]{0:T(128)}, f32[16]{0:T(128)}, f32[16]{0:T(128)}, f32[16]{0:T(128)}, f32[16]{0:T(128)}, /*index=5*/f32[16]{0:T(128)}) all-reduce(f32[16]{0:T(128)S(1)} %get-tuple-element.12, f32[16]{0:T(128)S(1)} %get-tuple-element.13, f32[16]{0:T(128)} %get-tuple-element.14, ...), channel_id=1, replica_groups=mesh['dp'=8,'vocab'=4] {'vocab'}, use_global_device_ids=true, to_apply=%region_21.22 | all-reduce | flops 96 | bytes 768 | tf_op jit(solution)/shard_map/psum | solution.py:14
  144.3 12.4 %all-reduce.1 = (f32[16]{0:T(128)S(1)}, f32[16]{0:T(128)S(1)}, f32[16]{0:T(128)S(1)}, f32[16]{0:T(128)S(1)}, f32[16]{0:T(128)}, /*index=5*/f32[16]{0:T(128)}) all-reduce(f32[16]{0:T(128)} %get-tuple-element.22, f32[16]{0:T(128)} %get-tuple-element.23, f32[16]{0:T(128)} %get-tuple-element.24, ...), channel_id=1, replica_groups=mesh['dp'=8,'vocab'=4] {'dp'}, use_global_device_ids=true, to_apply=%region_22.23 | all-reduce | flops 96 | bytes 768 | tf_op jit(solution)/shard_map/psum | solution.py:15
  156.8 0.7 subtract_bitcast_fusion.3
  157.4 0.1 subtract_bitcast_fusion.2
  157.5 0.1 subtract_bitcast_fusion.1
  157.6 0.7 copy.7
  (8 shorter events, 0.0 us)
Async XLA Ops:
  7.2 2.0 %copy-start = (bf16[384,4608]{1,0:T(8,128)(2,1)S(1)}, bf16[384,4608]{1,0:T(8,128)(2,1)}, u32[]{:S(2)}) copy-start(bf16[384,4608]{1,0:T(8,128)(2,1)} %param.6) | copy-start | bytes 10616836
  7.2 3.6 %copy-start.3 = (u32[32]{0:T(128)S(1)}, u32[32]{0:T(128)}, u32[]{:S(2)}) copy-start(u32[32]{0:T(128)} %constant.39) | copy-start | bytes 388
  7.2 59.0 %all-reduce.5.cloned.1.call-start = ((), (), s32[]{:S(2)}) async-start(), calls=%async_computation | async-start | bytes 884736
  100.6 2.6 %copy-start.2 = (bf16[1,2,4608]{2,1,0:T(2,128)(2,1)S(1)}, bf16[1,2,4608]{2,1,0:T(2,128)(2,1)}, u32[]{:S(2)}) copy-start(bf16[1,2,4608]{2,1,0:T(2,128)(2,1)} %get-tuple-element.32) | copy-start | bytes 55300
  114.4 2.6 %copy-start.1 = (bf16[1,2,4608]{2,1,0:T(2,128)(2,1)S(1)}, bf16[1,2,4608]{2,1,0:T(2,128)(2,1)}, u32[]{:S(2)}) copy-start(bf16[1,2,4608]{2,1,0:T(2,128)(2,1)} %get-tuple-element.34) | copy-start | bytes 55300
Sparse Core Ops, SparseCore 0:
  11.1 55.0 all-reduce.4
